TPU v7x, 32 devices: a whole 2x2x4 slice. The times are simulated.
32 devices in a mesh: mem: 8 (over z, x), grid: 4 (over y, core).
Axes of the slice: x: 2, y: 2, z: 4, core: 2. Of those that a mesh axis runs over, the one named last changes fastest.
Arguments:
- alpha: bfloat16 [16, 8, 768, 1536], P('mem', None, 'grid'), may hold values from -6 to 6
- perturbation: bfloat16 [16, 8, 768, 1536], P('mem', None, 'grid'), may hold values from -6 to 6
- legendre: bfloat16 [192, 128, 768], P('grid'), may hold values from -0.21875 to 0.21875
- response: float32 [192, 128], P('grid'), may hold values from 0.2 to 2
Outputs:
- increment: float32 [8, 768, 1536], P('mem', 'grid')
All inputs are finite; a program needn't handle non-finite values.
Results may differ from a plain program's by a relative error of at most 0.0063.
Values may be sent and summed in bfloat16 or wider, within the bound.
A program may use at most 128 MiB of HBM per device.

v0:
```python
import functools
import math

import jax
import jax.numpy as jnp
import numpy as np
from jax import lax
from jax.experimental import pallas as pl
from jax.experimental.pallas import tpu as pltpu
from jax.sharding import PartitionSpec as P


def build_table(lon_count, keep_dev, grid_count):
    col = np.arange(2 * keep_dev * grid_count)
    block = col // (2 * keep_dev)
    part = col // keep_dev % 2
    wave = block * keep_dev + col % keep_dev
    phase = wave[:, None] * np.arange(lon_count)[None, :] % lon_count
    angle = phase.astype(np.float32) * np.float32(2.0 * math.pi / lon_count)
    basis = np.where(part[:, None] == 0, np.cos(angle), np.sin(angle))
    return jnp.asarray(basis.astype(jnp.bfloat16))


def legendre_filter(split, legendre, response):
    coef = jnp.einsum("mnt,qmkit->qmkin", legendre, split, preferred_element_type=jnp.float32)
    coef = (coef * response[None, :, None, None, :]).astype(jnp.bfloat16)
    synth = jnp.einsum("mnt,qmkin->qmkit", legendre, coef, preferred_element_type=jnp.float32)
    return synth.astype(jnp.bfloat16)


def reduce_levels(partial, levels):
    mem_count = lax.axis_size("mem")
    me = lax.axis_index("mem")
    owned = levels // mem_count
    if mem_count % 2:
        every = jnp.concatenate([partial(i * owned, owned) for i in range(mem_count)])
        return lax.psum_scatter(every, "mem", scatter_dimension=0, tiled=True)
    ring = mem_count // 2
    side, place = me % 2, me // 2
    swap = [(j, j ^ 1) for j in range(mem_count)]
    onward = [(j, (j + 2) % mem_count) for j in range(mem_count)]
    total = None
    for step in range(ring):
        goal = (place + 2 * ring - 1 - step) % ring
        give = partial((2 * goal + 1 - side) * owned, owned).astype(jnp.bfloat16)
        got = lax.ppermute(give, "mem", swap)
        here = partial((2 * goal + side) * owned, owned)
        here = here + got.astype(jnp.float32)
        if total is not None:
            here = here + total.astype(jnp.float32)
        if step < ring - 1:
            total = lax.ppermute(here.astype(jnp.bfloat16), "mem", onward)
    return here


def filter_kernel(lat_dev, x_ref, legendre_ref, response_ref, out_ref, rows_ref, back_ref):
    grid_count, parts, waves, points = x_ref.shape
    tiles = points // 128
    per_pair = 2 * lat_dev // 128
    pairs = tiles // per_pair
    half = per_pair // 2
    for src in range(grid_count):
        for part in range(parts):
            for tile in range(tiles):
                spot = (tile % per_pair) * pairs + tile // per_pair
                rows_ref[src, part, spot * waves : (spot + 1) * waves, :] = x_ref[
                    src, part, :, tile * 128 : (tile + 1) * 128
                ].astype(jnp.float32)

    def one_wave(wave, carry):
        lines = []
        for part in range(parts):
            even, odd = [], []
            for src in range(grid_count):
                block = rows_ref[src, part, pl.ds(wave, tiles, stride=waves), :]
                piece = [block[i * pairs : (i + 1) * pairs] for i in range(per_pair)]
                even += piece[:half] + [piece[half][:, :64]]
                odd += [piece[half][:, 64:]] + piece[half + 1 :]
            lines += [jnp.concatenate(even, axis=1), jnp.concatenate(odd, axis=1)]
        field = jnp.concatenate(lines, axis=0).astype(jnp.bfloat16)
        basis = legendre_ref[wave]
        coef = lax.dot_general(
            field, basis, (((1,), (1,)), ((), ())), preferred_element_type=jnp.float32
        )
        coef = (coef * response_ref[pl.ds(wave, 1), :]).astype(jnp.bfloat16)
        synth = jnp.dot(coef, basis, preferred_element_type=jnp.float32)
        for part in range(parts):
            even = synth[2 * part * pairs : (2 * part + 1) * pairs]
            odd = synth[(2 * part + 1) * pairs : (2 * part + 2) * pairs]
            for src in range(grid_count):
                base = src * lat_dev
                both = jnp.concatenate(
                    [even[:, base : base + lat_dev], odd[:, base : base + lat_dev]], axis=1
                )
                block = jnp.concatenate(
                    [both[:, i * 128 : (i + 1) * 128] for i in range(per_pair)], axis=0
                )
                back_ref[src, part, pl.ds(wave, tiles, stride=waves), :] = block
        return carry

    lax.fori_loop(0, waves, one_wave, 0, unroll=4)
    for src in range(grid_count):
        for part in range(parts):
            for tile in range(tiles):
                spot = (tile % per_pair) * pairs + tile // per_pair
                out_ref[src, part, :, tile * 128 : (tile + 1) * 128] = back_ref[
                    src, part, spot * waves : (spot + 1) * waves, :
                ].astype(jnp.bfloat16)


def exchange_kernel(
    lat_dev, spectra_ref, legendre_ref, response_ref, result_ref,
    taken_ref, made_ref, basis_ref, rows_ref, back_ref,
    basis_sem, own_sem, send_sem, recv_sem, done_sem, back_send_sem, back_recv_sem,
):
    chunks, grid_count, _, waves, _ = taken_ref.shape
    me = lax.axis_index("grid")
    peers = [lax.rem(me + d, grid_count) for d in range(1, grid_count)]

    def basis_copy(c):
        return pltpu.make_async_copy(legendre_ref.at[c], basis_ref.at[c], basis_sem.at[c])

    def span(c):
        return pl.ds(pl.multiple_of(c * waves, waves), waves)

    def own_copy(c):
        return pltpu.make_async_copy(
            spectra_ref.at[me, :, span(c), :], taken_ref.at[c, me], own_sem.at[c]
        )

    def done_copy(c):
        return pltpu.make_async_copy(
            made_ref.at[c, me], result_ref.at[me, :, span(c), :], done_sem.at[c]
        )

    def out_copy(c, d):
        return pltpu.make_async_remote_copy(
            src_ref=spectra_ref.at[peers[d], :, span(c), :],
            dst_ref=taken_ref.at[c, me],
            send_sem=send_sem.at[c, d],
            recv_sem=recv_sem.at[c, d],
            device_id={"grid": peers[d]},
            device_id_type=pl.DeviceIdType.MESH,
        )

    def back_copy(c, d):
        return pltpu.make_async_remote_copy(
            src_ref=made_ref.at[c, peers[d]],
            dst_ref=result_ref.at[me, :, span(c), :],
            send_sem=back_send_sem.at[c, d],
            recv_sem=back_recv_sem.at[c, d],
            device_id={"grid": peers[d]},
            device_id_type=pl.DeviceIdType.MESH,
        )

    for c in range(chunks):
        basis_copy(c).start()
        own_copy(c).start()
    barrier = pltpu.get_barrier_semaphore()
    for peer in peers:
        pl.semaphore_signal(
            barrier, inc=1, device_id={"grid": peer}, device_id_type=pl.DeviceIdType.MESH
        )
    pl.semaphore_wait(barrier, grid_count - 1)
    for c in range(chunks):
        for d in range(grid_count - 1):
            out_copy(c, d).start()

    def one_chunk(c, carry):
        basis_copy(c).wait()
        own_copy(c).wait()
        for d in range(grid_count - 1):
            out_copy(c, d).wait_recv()
        filter_kernel(
            lat_dev, taken_ref.at[c], basis_ref.at[c], response_ref.at[c], made_ref.at[c], rows_ref, back_ref
        )
        done_copy(c).start()
        for d in range(grid_count - 1):
            back_copy(c, d).start()
        return carry

    lax.fori_loop(0, chunks, one_chunk, 0)
    for c in range(chunks):
        done_copy(c).wait()
        for d in range(grid_count - 1):
            out_copy(c, d).wait_send()
            back_copy(c, d).wait()


def filter_exchanged(spectra, legendre, response, lat_dev):
    grid_count, parts, keep_dev, points = spectra.shape
    degrees, lat_count = legendre.shape[1:]
    waves = 16
    chunks = keep_dev // waves
    stage = pltpu.VMEM((chunks, grid_count, parts, waves, points), jnp.bfloat16)
    turned = pltpu.VMEM((grid_count, parts, points // 128 * waves, 128), jnp.float32)
    one = pltpu.SemaphoreType.DMA((chunks,))
    each = pltpu.SemaphoreType.DMA((chunks, grid_count - 1))
    return pl.pallas_call(
        functools.partial(exchange_kernel, lat_dev),
        out_shape=jax.ShapeDtypeStruct(spectra.shape, jnp.bfloat16),
        in_specs=[
            pl.BlockSpec(memory_space=pl.ANY),
            pl.BlockSpec(memory_space=pl.ANY),
            pl.BlockSpec(memory_space=pltpu.VMEM),
        ],
        out_specs=pl.BlockSpec(memory_space=pl.ANY),
        scratch_shapes=[
            stage, stage, pltpu.VMEM((chunks, waves, degrees, lat_count), jnp.bfloat16), turned, turned,
            one, one, each, each, one, each, each,
        ],
        compiler_params=pltpu.CompilerParams(
            vmem_limit_bytes=56 * 2**20, collective_id=0, has_side_effects=True
        ),
        cost_estimate=pl.CostEstimate(
            flops=2**35, bytes_accessed=2 * keep_dev * degrees * lat_count, transcendentals=0
        ),
    )(
        spectra,
        legendre.reshape(chunks, waves, degrees, lat_count),
        response.reshape(chunks, waves, degrees),
    )


def synth_kernel(where_ref, field_ref, table_ref, weight_ref, give_ref, keep_ref, total_ref):
    member = pl.program_id(1)
    side = where_ref[1]
    pair, lat_dev, wide = total_ref.shape
    values = lax.dot_general(
        field_ref[...], table_ref[...], (((0,), (0,)), ((), ())), preferred_element_type=jnp.float32
    ).reshape(pair, lat_dev, wide)
    term = values * weight_ref[0].astype(jnp.float32)

    @pl.when(member == 0)
    def _():
        total_ref[...] = term

    @pl.when(member > 0)
    def _():
        total_ref[...] += term

    @pl.when(member == pl.num_programs(1) - 1)
    def _():
        give_ref[0] = total_ref[1 - side].astype(jnp.bfloat16)
        keep_ref[0] = total_ref[side]


def synth_pair(filtered, table, perturbation, goal, side, strip, strips):
    mem_dev, levels, lat_dev, lon_count = perturbation.shape
    cols = table.shape[0]
    pairs = levels // 2
    strip_lon = lon_count // strips
    wide = strip_lon
    first = strip * (strip_lon // wide)
    level = pl.BlockSpec((1, lat_dev, wide), lambda i, k, w: (0, 0, i))
    return pl.pallas_call(
        synth_kernel,
        out_shape=(
            jax.ShapeDtypeStruct((1, lat_dev, strip_lon), jnp.bfloat16),
            jax.ShapeDtypeStruct((1, lat_dev, strip_lon), jnp.float32),
        ),
        grid_spec=pltpu.PrefetchScalarGridSpec(
            num_scalar_prefetch=1,
            grid=(strip_lon // wide, mem_dev),
            in_specs=[
                pl.BlockSpec((cols, 2 * lat_dev), lambda i, k, w: (0, k * pairs + w[0])),
                pl.BlockSpec((cols, wide), lambda i, k, w: (0, i + first)),
                pl.BlockSpec((1, 2, lat_dev, wide), lambda i, k, w: (k, w[0], 0, i + first)),
            ],
            out_specs=(level, level),
            scratch_shapes=[pltpu.VMEM((2, lat_dev, wide), jnp.float32)],
        ),
        compiler_params=pltpu.CompilerParams(vmem_limit_bytes=56 * 2**20),
        cost_estimate=pl.CostEstimate(
            flops=4 * mem_dev * lat_dev * cols * strip_lon,
            bytes_accessed=4 * mem_dev * lat_dev * strip_lon,
            transcendentals=0,
        ),
    )(jnp.stack([goal, side]).astype(jnp.int32), filtered, table, perturbation)


def reduce_pairs(both, strips):
    mem_count = lax.axis_size("mem")
    me = lax.axis_index("mem")
    ring = mem_count // 2
    side, place = me % 2, me // 2
    swap = [(j, j ^ 1) for j in range(mem_count)]
    onward = [(j, (j + 2) % mem_count) for j in range(mem_count)]
    totals = [None] * strips
    for step in range(ring):
        goal = (place + 2 * ring - 1 - step) % ring
        for strip in range(strips):
            give, here = both(goal, side, strip)
            here = here + lax.ppermute(give, "mem", swap).astype(jnp.float32)
            if step > 0:
                here = here + totals[strip].astype(jnp.float32)
            if step < ring - 1:
                here = lax.ppermute(here.astype(jnp.bfloat16), "mem", onward)
            totals[strip] = here
    return jnp.concatenate(totals, axis=2)


def packed(alpha, perturbation, legendre, response, table):
    mem_dev, levels, lat_dev, lon_count = alpha.shape
    keep_dev = legendre.shape[0]
    grid_count = lax.axis_size("grid")
    points = mem_dev * levels * lat_dev
    spectra = lax.dot_general(
        table, alpha.reshape(points, lon_count), (((1,), (1,)), ((), ())), preferred_element_type=jnp.float32
    ).astype(jnp.bfloat16)
    spectra = spectra.reshape(grid_count, 2, keep_dev, points)
    filtered = filter_exchanged(spectra, legendre, response, lat_dev)
    filtered = filtered.reshape(grid_count * 2 * keep_dev, points)
    strips = 2 if lon_count % 256 == 0 else 1

    def both(goal, side, strip):
        return synth_pair(filtered, table, perturbation, goal, side, strip, strips)

    return reduce_pairs(both, strips)


def body(alpha, perturbation, legendre, response):
    mem_dev, levels, lat_dev, lon_count = alpha.shape
    keep_dev = legendre.shape[0]
    grid_count = lax.axis_size("grid")
    members = mem_dev * lax.axis_size("mem")
    cols = 2 * keep_dev
    table = build_table(lon_count, keep_dev, grid_count)
    wave = lax.axis_index("grid") * keep_dev + jnp.arange(keep_dev)
    response = response * jnp.where(wave == 0, 1.0, 2.0).astype(jnp.float32)[:, None]

    scale = jnp.float32(1.0 / (lon_count * math.sqrt(members - 1)))
    if keep_dev % 16 == 0 and lat_dev % 128 == 64 and levels == lax.axis_size("mem") and levels % 2 == 0:
        return packed(alpha, perturbation, legendre, response, table) * scale

    points = mem_dev * levels * lat_dev
    lane = math.gcd(points, 128)
    spectra = jnp.einsum("cx,klyx->ckly", table, alpha, preferred_element_type=jnp.float32)
    spectra = spectra.astype(jnp.bfloat16).reshape(grid_count, cols, points // lane, lane)
    spectra = lax.all_to_all(spectra, "grid", split_axis=0, concat_axis=0, tiled=True)
    split = spectra.reshape(grid_count, 2, keep_dev, mem_dev, levels, lat_dev)
    split = jnp.transpose(split, (1, 2, 3, 4, 0, 5)).reshape(2, keep_dev, mem_dev, levels, -1)
    filtered = legendre_filter(split, legendre, response)
    filtered = filtered.reshape(2, keep_dev, mem_dev, levels, grid_count, lat_dev)
    filtered = jnp.transpose(filtered, (4, 0, 1, 2, 3, 5)).reshape(grid_count, cols, points // lane, lane)
    filtered = lax.all_to_all(filtered, "grid", split_axis=0, concat_axis=0, tiled=True)
    filtered = filtered.reshape(grid_count * cols, mem_dev, levels, lat_dev)
    filtered = jnp.transpose(filtered, (1, 2, 3, 0))

    def partial(level, count):
        field = lax.dynamic_slice_in_dim(filtered, level, count, 1)
        weight = lax.dynamic_slice_in_dim(perturbation, level, count, 1)
        values = jnp.einsum("klyc,cx->klyx", field, table, preferred_element_type=jnp.float32)
        return jnp.sum(values * weight, axis=0)

    total = reduce_levels(partial, levels)
    return total * scale


def solution(mesh):
    placed = (
        P("mem", None, "grid", None),
        P("mem", None, "grid", None),
        P("grid", None, None),
        P("grid", None),
    )
    return jax.shard_map(
        body, mesh=mesh, in_specs=placed, out_specs=P("mem", "grid", None), check_vma=False
    )
```

profile of v0, /device:TPU:0, one launch (start us, length us, event | category | flops | bytes accessed | tf_op | source)
XLA Modules:
  0.0 137.6 jit_solution(10986242600484354565)
XLA Ops:
  0.0 1.4 %broadcast_multiply_fusion = f32[48,128]{1,0:T(8,128)} fusion(f32[48,128]{1,0:T(8,128)} %param.8, f32[48]{0:T(128)S(1)} %compare_select_fusion), kind=kLoop, calls=%fused_computation.10 | loop fusion | flops 6144 | bytes 49344 | tf_op jit(solution)/shard_map/mul | solution.py:330
  1.4 9.3 %convolution_convert_fusion = bf16[384,3072]{1,0:T(8,128)(2,1)} fusion(bf16[384,1536]{1,0:T(8,128)(2,1)} %constant.80.clone.table_ref, bf16[3072,1536]{1,0:T(8,128)(2,1)} %bitcast.21), kind=kOutput, calls=%fused_computation | convolution fusion | flops 3625058304 | bytes 12976128 | tf_op jit(solution)/shard_map/dot_general | solution.py:308
  10.8 0.7 pad_add_fusion.2
  11.4 55.4 %shard_map.55 = bf16[4,2,48,3072]{3,2,1,0:T(8,128)(2,1)} custom-call(bf16[4,2,48,3072]{3,2,1,0:T(8,128)(2,1)} %bitcast.23, bf16[3,16,128,768]{3,2,1,0:T(8,128)(2,1)} %bitcast.22, f32[3,16,128]{2,1,0:T(8,128)} %bitcast.20), custom_call_target="tpu_custom_call" | custom-call | flops 34359738368 | bytes 9437184 | tf_op jit(solution)/shard_map/pallas_call | solution.py:199
  66.9 4.2 %shard_map.63 = (bf16[1,192,768]{2,1,0:T(8,128)(2,1)}, f32[1,192,768]{2,1,0:T(8,128)}) custom-call(s32[2]{0:T(128)} %get-tuple-element.40.where_ref, bf16[384,3072]{1,0:T(8,128)(2,1)} %bitcast.12, bf16[384,1536]{1,0:T(8,128)(2,1)} %constant.80.clone.table_ref, bf16[2,8,192,1536]{3,2,1,0:T(8,128)(2,1)} %weight_ref.15), custom_call_target="tpu_custom_call" | custom-call | flops 452984832 | bytes 1179648 | tf_op jit(solution)/shard_map/pallas_call | solution.py:256
  71.1 1.5 %collective-permute-start.10 = (bf16[1,192,768]{2,1,0:T(8,128)(2,1)}, bf16[1,192,768]{2,1,0:T(8,128)(2,1)S(1)}, u32[]{:S(2)}, u32[]{:S(2)}) collective-permute-start(bf16[1,192,768]{2,1,0:T(8,128)(2,1)} %get-tuple-element.36), channel_id=1, source_target_pairs={{0,4},{4,0},{8,12},{12,8},{16,20},{20,16},{24,28},{28,24},{1,5},{5... | collective-permute-start | bytes 884744 | tf_op jit(solution)/shard_map/ppermute | solution.py:294
  72.6 4.2 %shard_map.59 = (bf16[1,192,768]{2,1,0:T(8,128)(2,1)}, f32[1,192,768]{2,1,0:T(8,128)}) custom-call(s32[2]{0:T(128)} %get-tuple-element.40.where_ref, bf16[384,3072]{1,0:T(8,128)(2,1)} %bitcast.13, bf16[384,1536]{1,0:T(8,128)(2,1)} %constant.80.clone.table_ref, bf16[2,8,192,1536]{3,2,1,0:T(8,128)(2,1)} %weight_ref.15), custom_call_target="tpu_custom_call" | custom-call | flops 452984832 | bytes 1179648 | tf_op jit(solution)/shard_map/pallas_call | solution.py:256
  76.8 0.5 collective-permute-start.3
  77.4 4.2 %shard_map.62 = (bf16[1,192,768]{2,1,0:T(8,128)(2,1)}, f32[1,192,768]{2,1,0:T(8,128)}) custom-call(s32[2]{0:T(128)} %get-tuple-element.39.where_ref, bf16[384,3072]{1,0:T(8,128)(2,1)} %bitcast.14, bf16[384,1536]{1,0:T(8,128)(2,1)} %constant.80.clone.table_ref, bf16[2,8,192,1536]{3,2,1,0:T(8,128)(2,1)} %weight_ref.15), custom_call_target="tpu_custom_call" | custom-call | flops 452984832 | bytes 1179648 | tf_op jit(solution)/shard_map/pallas_call | solution.py:256
  81.6 1.5 %collective-permute-start.9 = (bf16[1,192,768]{2,1,0:T(8,128)(2,1)}, bf16[1,192,768]{2,1,0:T(8,128)(2,1)S(1)}, u32[]{:S(2)}, u32[]{:S(2)}) collective-permute-start(bf16[1,192,768]{2,1,0:T(8,128)(2,1)} %get-tuple-element.34), channel_id=1, source_target_pairs={{0,4},{4,0},{8,12},{12,8},{16,20},{20,16},{24,28},{28,24},{1,5},{5... | collective-permute-start | bytes 884744 | tf_op jit(solution)/shard_map/ppermute | solution.py:294
  83.1 4.3 %shard_map.58 = (bf16[1,192,768]{2,1,0:T(8,128)(2,1)}, f32[1,192,768]{2,1,0:T(8,128)}) custom-call(s32[2]{0:T(128)} %get-tuple-element.39.where_ref, bf16[384,3072]{1,0:T(8,128)(2,1)} %bitcast.15, bf16[384,1536]{1,0:T(8,128)(2,1)} %constant.80.clone.table_ref, bf16[2,8,192,1536]{3,2,1,0:T(8,128)(2,1)} %weight_ref.15), custom_call_target="tpu_custom_call" | custom-call | flops 452984832 | bytes 1179648 | tf_op jit(solution)/shard_map/pallas_call | solution.py:256
  87.3 0.5 collective-permute-start.2
  87.9 0.6 pad_add_fusion
  88.5 4.4 %shard_map.61 = (bf16[1,192,768]{2,1,0:T(8,128)(2,1)}, f32[1,192,768]{2,1,0:T(8,128)}) custom-call(s32[2]{0:T(128)} %get-tuple-element.38.where_ref, bf16[384,3072]{1,0:T(8,128)(2,1)} %bitcast.16, bf16[384,1536]{1,0:T(8,128)(2,1)} %constant.80.clone.table_ref, bf16[2,8,192,1536]{3,2,1,0:T(8,128)(2,1)} %weight_ref.15), custom_call_target="tpu_custom_call" | custom-call | flops 452984832 | bytes 1179648 | tf_op jit(solution)/shard_map/pallas_call | solution.py:256
  92.8 1.5 %collective-permute-start.8 = (bf16[1,192,768]{2,1,0:T(8,128)(2,1)}, bf16[1,192,768]{2,1,0:T(8,128)(2,1)S(1)}, u32[]{:S(2)}, u32[]{:S(2)}) collective-permute-start(bf16[1,192,768]{2,1,0:T(8,128)(2,1)} %get-tuple-element.32), channel_id=1, source_target_pairs={{0,4},{4,0},{8,12},{12,8},{16,20},{20,16},{24,28},{28,24},{1,5},{5... | collective-permute-start | bytes 884744 | tf_op jit(solution)/shard_map/ppermute | solution.py:294
  94.3 0.0 collective-permute-done.10
  94.3 0.0 copy-done.3
  94.3 0.1 add_convert_fusion.2
  94.4 0.0 copy-start.2
  94.4 0.0 copy-start.5
  94.4 1.6 %collective-permute-start.11 = (bf16[1,192,768]{2,1,0:T(8,128)(2,1)S(1)}, bf16[1,192,768]{2,1,0:T(8,128)(2,1)S(1)}, u32[]{:S(2)}, u32[]{:S(2)}) collective-permute-start(bf16[1,192,768]{2,1,0:T(8,128)(2,1)S(1)} %add_convert_fusion.2), channel_id=1, source_target_pairs={{0,8},{4,12},{8,16},{12,20},{16,24},{20,28},{24,0},{28,4},{1,9},{5... | collective-permute-start | bytes 884744 | tf_op jit(solution)/shard_map/ppermute | solution.py:298
  96.0 4.3 %shard_map.57 = (bf16[1,192,768]{2,1,0:T(8,128)(2,1)}, f32[1,192,768]{2,1,0:T(8,128)}) custom-call(s32[2]{0:T(128)} %get-tuple-element.38.where_ref, bf16[384,3072]{1,0:T(8,128)(2,1)} %bitcast.17, bf16[384,1536]{1,0:T(8,128)(2,1)} %constant.80.clone.table_ref, bf16[2,8,192,1536]{3,2,1,0:T(8,128)(2,1)} %weight_ref.15), custom_call_target="tpu_custom_call" | custom-call | flops 452984832 | bytes 1179648 | tf_op jit(solution)/shard_map/pallas_call | solution.py:256
  100.3 0.0 collective-permute-done.3
  100.3 0.5 collective-permute-start.1
  100.9 0.0 copy-done.2
  100.9 0.1 add_convert_fusion.5
  100.9 0.0 collective-permute-done.9
  100.9 1.6 %collective-permute-start.4 = (bf16[1,192,768]{2,1,0:T(8,128)(2,1)S(1)}, bf16[1,192,768]{2,1,0:T(8,128)(2,1)S(1)}, u32[]{:S(2)}, u32[]{:S(2)}) collective-permute-start(bf16[1,192,768]{2,1,0:T(8,128)(2,1)S(1)} %add_convert_fusion.5), channel_id=1, source_target_pairs={{0,8},{4,12},{8,16},{12,20},{16,24},{20,28},{24,0},{28,4},{1,9},{5... | collective-permute-start | bytes 884744 | tf_op jit(solution)/shard_map/ppermute | solution.py:298
  102.6 2.6 %collective-permute-done.11 = bf16[1,192,768]{2,1,0:T(8,128)(2,1)S(1)} collective-permute-done((bf16[1,192,768]{2,1,0:T(8,128)(2,1)S(1)}, bf16[1,192,768]{2,1,0:T(8,128)(2,1)S(1)}, u32[]{:S(2)}, u32[]{:S(2)}) %collective-permute-start.11) | collective-permute-done | bytes 294944 | tf_op jit(solution)/shard_map/ppermute | solution.py:298
  105.2 0.0 copy-done.5
  105.2 0.1 add_convert_fusion.1
  105.2 0.1 collective-permute-start.12
  105.3 0.0 copy-start.4
  105.3 0.0 copy-start.7
  105.3 4.4 %shard_map.60 = (bf16[1,192,768]{2,1,0:T(8,128)(2,1)}, f32[1,192,768]{2,1,0:T(8,128)}) custom-call(s32[2]{0:T(128)} %get-tuple-element.37.where_ref, bf16[384,3072]{1,0:T(8,128)(2,1)} %bitcast.18, bf16[384,1536]{1,0:T(8,128)(2,1)} %constant.80.clone.table_ref, bf16[2,8,192,1536]{3,2,1,0:T(8,128)(2,1)} %weight_ref.15), custom_call_target="tpu_custom_call" | custom-call | flops 452984832 | bytes 1179648 | tf_op jit(solution)/shard_map/pallas_call | solution.py:256
  109.7 0.0 collective-permute-done.2
  109.7 0.5 collective-permute-start.7
  110.2 2.5 %collective-permute-done.4 = bf16[1,192,768]{2,1,0:T(8,128)(2,1)S(1)} collective-permute-done((bf16[1,192,768]{2,1,0:T(8,128)(2,1)S(1)}, bf16[1,192,768]{2,1,0:T(8,128)(2,1)S(1)}, u32[]{:S(2)}, u32[]{:S(2)}) %collective-permute-start.4) | collective-permute-done | bytes 294944 | tf_op jit(solution)/shard_map/ppermute | solution.py:298
  112.7 0.0 copy-done.4
  112.7 0.1 add_convert_fusion.4
  112.8 0.1 collective-permute-start.5
  112.8 0.0 collective-permute-done.8
  112.8 6.1 %collective-permute-done.12 = bf16[1,192,768]{2,1,0:T(8,128)(2,1)S(1)} collective-permute-done((bf16[1,192,768]{2,1,0:T(8,128)(2,1)S(1)}, bf16[1,192,768]{2,1,0:T(8,128)(2,1)S(1)}, u32[]{:S(2)}, u32[]{:S(2)}) %collective-permute-start.12) | collective-permute-done | bytes 294944 | tf_op jit(solution)/shard_map/ppermute | solution.py:298
  119.0 0.0 copy-done.7
  119.0 0.1 add_convert_fusion
  119.1 0.0 copy-start.6
  119.1 0.0 copy-start
  119.1 0.1 collective-permute-start.13
  119.2 4.4 %shard_map.56 = (bf16[1,192,768]{2,1,0:T(8,128)(2,1)}, f32[1,192,768]{2,1,0:T(8,128)}) custom-call(s32[2]{0:T(128)} %get-tuple-element.37.where_ref, bf16[384,3072]{1,0:T(8,128)(2,1)} %bitcast.19, bf16[384,1536]{1,0:T(8,128)(2,1)} %constant.80.clone.table_ref, bf16[2,8,192,1536]{3,2,1,0:T(8,128)(2,1)} %weight_ref.15), custom_call_target="tpu_custom_call" | custom-call | flops 452984832 | bytes 1179648 | tf_op jit(solution)/shard_map/pallas_call | solution.py:256
  123.6 1.5 %collective-permute-start = (bf16[1,192,768]{2,1,0:T(8,128)(2,1)}, bf16[1,192,768]{2,1,0:T(8,128)(2,1)S(1)}, u32[]{:S(2)}, u32[]{:S(2)}) collective-permute-start(bf16[1,192,768]{2,1,0:T(8,128)(2,1)} %get-tuple-element.22), channel_id=1, source_target_pairs={{0,4},{4,0},{8,12},{12,8},{16,20},{20,16},{24,28},{28,24},{1,5},{5... | collective-permute-start | bytes 884744 | tf_op jit(solution)/shard_map/ppermute | solution.py:294
  125.1 0.0 collective-permute-done.1
  125.1 0.2 collective-permute-done.5
  125.3 0.0 copy-done.6
  125.3 0.1 add_convert_fusion.3
  125.4 1.0 collective-permute-start.6
  126.4 0.0 collective-permute-done.7
  126.4 5.2 %collective-permute-done.13 = bf16[1,192,768]{2,1,0:T(8,128)(2,1)S(1)} collective-permute-done((bf16[1,192,768]{2,1,0:T(8,128)(2,1)S(1)}, bf16[1,192,768]{2,1,0:T(8,128)(2,1)S(1)}, u32[]{:S(2)}, u32[]{:S(2)}) %collective-permute-start.13) | collective-permute-done | bytes 294944 | tf_op jit(solution)/shard_map/ppermute | solution.py:298
  131.6 0.0 copy-done
  131.6 0.1 convert_add_fusion
  131.7 0.0 collective-permute-done
  131.7 4.6 %collective-permute-done.6 = bf16[1,192,768]{2,1,0:T(8,128)(2,1)S(1)} collective-permute-done((bf16[1,192,768]{2,1,0:T(8,128)(2,1)S(1)}, bf16[1,192,768]{2,1,0:T(8,128)(2,1)S(1)}, u32[]{:S(2)}, u32[]{:S(2)}) %collective-permute-start.6) | collective-permute-done | bytes 294944 | tf_op jit(solution)/shard_map/ppermute | solution.py:298
  136.3 0.0 copy-done.1
  136.3 0.1 convert_add_fusion.1
  136.4 1.2 maximum_multiply_fusion
  (3 shorter events, 0.0 us)
Async XLA Ops:
  71.1 23.2 %collective-permute-start.10 = (bf16[1,192,768]{2,1,0:T(8,128)(2,1)}, bf16[1,192,768]{2,1,0:T(8,128)(2,1)S(1)}, u32[]{:S(2)}, u32[]{:S(2)}) collective-permute-start(bf16[1,192,768]{2,1,0:T(8,128)(2,1)} %get-tuple-element.36), channel_id=1, source_target_pairs={{0,4},{4,0},{8,12},{12,8},{16,20},{20,16},{24,28},{28,24},{1,5},{5... | collective-permute-start | bytes 884744 | tf_op jit(solution)/shard_map/ppermute | solution.py:294
  76.8 23.5 %collective-permute-start.3 = (bf16[1,192,768]{2,1,0:T(8,128)(2,1)}, bf16[1,192,768]{2,1,0:T(8,128)(2,1)S(1)}, u32[]{:S(2)}, u32[]{:S(2)}) collective-permute-start(bf16[1,192,768]{2,1,0:T(8,128)(2,1)} %get-tuple-element.28), channel_id=1, source_target_pairs={{0,4},{4,0},{8,12},{12,8},{16,20},{20,16},{24,28},{28,24},{1,5},{5... | collective-permute-start | bytes 884744 | tf_op jit(solution)/shard_map/ppermute | solution.py:294
  81.6 19.3 %collective-permute-start.9 = (bf16[1,192,768]{2,1,0:T(8,128)(2,1)}, bf16[1,192,768]{2,1,0:T(8,128)(2,1)S(1)}, u32[]{:S(2)}, u32[]{:S(2)}) collective-permute-start(bf16[1,192,768]{2,1,0:T(8,128)(2,1)} %get-tuple-element.34), channel_id=1, source_target_pairs={{0,4},{4,0},{8,12},{12,8},{16,20},{20,16},{24,28},{28,24},{1,5},{5... | collective-permute-start | bytes 884744 | tf_op jit(solution)/shard_map/ppermute | solution.py:294
  87.3 22.4 %collective-permute-start.2 = (bf16[1,192,768]{2,1,0:T(8,128)(2,1)}, bf16[1,192,768]{2,1,0:T(8,128)(2,1)S(1)}, u32[]{:S(2)}, u32[]{:S(2)}) collective-permute-start(bf16[1,192,768]{2,1,0:T(8,128)(2,1)} %get-tuple-element.26), channel_id=1, source_target_pairs={{0,4},{4,0},{8,12},{12,8},{16,20},{20,16},{24,28},{28,24},{1,5},{5... | collective-permute-start | bytes 884744 | tf_op jit(solution)/shard_map/ppermute | solution.py:294
  88.5 5.9 %copy-start.3 = (f32[1,192,768]{2,1,0:T(8,128)S(1)}, f32[1,192,768]{2,1,0:T(8,128)}, u32[]{:S(2)}) copy-start(f32[1,192,768]{2,1,0:T(8,128)} %get-tuple-element.35) | copy-start | bytes 1769476
  92.8 20.0 %collective-permute-start.8 = (bf16[1,192,768]{2,1,0:T(8,128)(2,1)}, bf16[1,192,768]{2,1,0:T(8,128)(2,1)S(1)}, u32[]{:S(2)}, u32[]{:S(2)}) collective-permute-start(bf16[1,192,768]{2,1,0:T(8,128)(2,1)} %get-tuple-element.32), channel_id=1, source_target_pairs={{0,4},{4,0},{8,12},{12,8},{16,20},{20,16},{24,28},{28,24},{1,5},{5... | collective-permute-start | bytes 884744 | tf_op jit(solution)/shard_map/ppermute | solution.py:294
  94.4 6.5 %copy-start.2 = (f32[1,192,768]{2,1,0:T(8,128)S(1)}, f32[1,192,768]{2,1,0:T(8,128)}, u32[]{:S(2)}) copy-start(f32[1,192,768]{2,1,0:T(8,128)} %get-tuple-element.27) | copy-start | bytes 1769476
  94.4 10.7 %copy-start.5 = (f32[1,192,768]{2,1,0:T(8,128)S(1)}, f32[1,192,768]{2,1,0:T(8,128)}, u32[]{:S(2)}) copy-start(f32[1,192,768]{2,1,0:T(8,128)} %get-tuple-element.33) | copy-start | bytes 1769476
  94.4 10.7 %collective-permute-start.11 = (bf16[1,192,768]{2,1,0:T(8,128)(2,1)S(1)}, bf16[1,192,768]{2,1,0:T(8,128)(2,1)S(1)}, u32[]{:S(2)}, u32[]{:S(2)}) collective-permute-start(bf16[1,192,768]{2,1,0:T(8,128)(2,1)S(1)} %add_convert_fusion.2), channel_id=1, source_target_pairs={{0,8},{4,12},{8,16},{12,20},{16,24},{20,28},{24,0},{28,4},{1,9},{5... | collective-permute-start | bytes 884744 | tf_op jit(solution)/shard_map/ppermute | solution.py:298
  100.3 24.7 %collective-permute-start.1 = (bf16[1,192,768]{2,1,0:T(8,128)(2,1)}, bf16[1,192,768]{2,1,0:T(8,128)(2,1)S(1)}, u32[]{:S(2)}, u32[]{:S(2)}) collective-permute-start(bf16[1,192,768]{2,1,0:T(8,128)(2,1)} %get-tuple-element.24), channel_id=1, source_target_pairs={{0,4},{4,0},{8,12},{12,8},{16,20},{20,16},{24,28},{28,24},{1,5},{5... | collective-permute-start | bytes 884744 | tf_op jit(solution)/shard_map/ppermute | solution.py:294
  100.9 11.7 %collective-permute-start.4 = (bf16[1,192,768]{2,1,0:T(8,128)(2,1)S(1)}, bf16[1,192,768]{2,1,0:T(8,128)(2,1)S(1)}, u32[]{:S(2)}, u32[]{:S(2)}) collective-permute-start(bf16[1,192,768]{2,1,0:T(8,128)(2,1)S(1)} %add_convert_fusion.5), channel_id=1, source_target_pairs={{0,8},{4,12},{8,16},{12,20},{16,24},{20,28},{24,0},{28,4},{1,9},{5... | collective-permute-start | bytes 884744 | tf_op jit(solution)/shard_map/ppermute | solution.py:298
  105.2 13.7 %collective-permute-start.12 = (bf16[1,192,768]{2,1,0:T(8,128)(2,1)S(1)}, bf16[1,192,768]{2,1,0:T(8,128)(2,1)S(1)}, u32[]{:S(2)}, u32[]{:S(2)}) collective-permute-start(bf16[1,192,768]{2,1,0:T(8,128)(2,1)S(1)} %add_convert_fusion.1), channel_id=1, source_target_pairs={{0,8},{4,12},{8,16},{12,20},{16,24},{20,28},{24,0},{28,4},{1,9},{5... | collective-permute-start | bytes 884744 | tf_op jit(solution)/shard_map/ppermute | solution.py:298
  105.3 7.4 %copy-start.4 = (f32[1,192,768]{2,1,0:T(8,128)S(1)}, f32[1,192,768]{2,1,0:T(8,128)}, u32[]{:S(2)}) copy-start(f32[1,192,768]{2,1,0:T(8,128)} %get-tuple-element.25) | copy-start | bytes 1769476
  105.3 13.7 %copy-start.7 = (f32[1,192,768]{2,1,0:T(8,128)S(1)}, f32[1,192,768]{2,1,0:T(8,128)}, u32[]{:S(2)}) copy-start(f32[1,192,768]{2,1,0:T(8,128)} %get-tuple-element.31) | copy-start | bytes 1769476
  109.7 16.7 %collective-permute-start.7 = (bf16[1,192,768]{2,1,0:T(8,128)(2,1)}, bf16[1,192,768]{2,1,0:T(8,128)(2,1)S(1)}, u32[]{:S(2)}, u32[]{:S(2)}) collective-permute-start(bf16[1,192,768]{2,1,0:T(8,128)(2,1)} %get-tuple-element.30), channel_id=1, source_target_pairs={{0,4},{4,0},{8,12},{12,8},{16,20},{20,16},{24,28},{28,24},{1,5},{5... | collective-permute-start | bytes 884744 | tf_op jit(solution)/shard_map/ppermute | solution.py:294
  112.8 12.5 %collective-permute-start.5 = (bf16[1,192,768]{2,1,0:T(8,128)(2,1)S(1)}, bf16[1,192,768]{2,1,0:T(8,128)(2,1)S(1)}, u32[]{:S(2)}, u32[]{:S(2)}) collective-permute-start(bf16[1,192,768]{2,1,0:T(8,128)(2,1)S(1)} %add_convert_fusion.4), channel_id=1, source_target_pairs={{0,8},{4,12},{8,16},{12,20},{16,24},{20,28},{24,0},{28,4},{1,9},{5... | collective-permute-start | bytes 884744 | tf_op jit(solution)/shard_map/ppermute | solution.py:298
  119.1 6.2 %copy-start.6 = (f32[1,192,768]{2,1,0:T(8,128)S(1)}, f32[1,192,768]{2,1,0:T(8,128)}, u32[]{:S(2)}) copy-start(f32[1,192,768]{2,1,0:T(8,128)} %get-tuple-element.23) | copy-start | bytes 1769476
  119.1 12.5 %copy-start = (f32[1,192,768]{2,1,0:T(8,128)S(1)}, f32[1,192,768]{2,1,0:T(8,128)}, u32[]{:S(2)}) copy-start(f32[1,192,768]{2,1,0:T(8,128)} %get-tuple-element.29) | copy-start | bytes 1769476
  119.1 12.5 %collective-permute-start.13 = (bf16[1,192,768]{2,1,0:T(8,128)(2,1)S(1)}, bf16[1,192,768]{2,1,0:T(8,128)(2,1)S(1)}, u32[]{:S(2)}, u32[]{:S(2)}) collective-permute-start(bf16[1,192,768]{2,1,0:T(8,128)(2,1)S(1)} %add_convert_fusion), channel_id=1, source_target_pairs={{0,8},{4,12},{8,16},{12,20},{16,24},{20,28},{24,0},{28,4},{1,9},{5... | collective-permute-start | bytes 884744 | tf_op jit(solution)/shard_map/ppermute | solution.py:298
  123.6 12.8 %copy-start.1 = (f32[1,192,768]{2,1,0:T(8,128)S(1)}, f32[1,192,768]{2,1,0:T(8,128)}, u32[]{:S(2)}) copy-start(f32[1,192,768]{2,1,0:T(8,128)} %get-tuple-element.21) | copy-start | bytes 1769476
  123.6 8.1 %collective-permute-start = (bf16[1,192,768]{2,1,0:T(8,128)(2,1)}, bf16[1,192,768]{2,1,0:T(8,128)(2,1)S(1)}, u32[]{:S(2)}, u32[]{:S(2)}) collective-permute-start(bf16[1,192,768]{2,1,0:T(8,128)(2,1)} %get-tuple-element.22), channel_id=1, source_target_pairs={{0,4},{4,0},{8,12},{12,8},{16,20},{20,16},{24,28},{28,24},{1,5},{5... | collective-permute-start | bytes 884744 | tf_op jit(solution)/shard_map/ppermute | solution.py:294
  125.4 10.9 %collective-permute-start.6 = (bf16[1,192,768]{2,1,0:T(8,128)(2,1)S(1)}, bf16[1,192,768]{2,1,0:T(8,128)(2,1)S(1)}, u32[]{:S(2)}, u32[]{:S(2)}) collective-permute-start(bf16[1,192,768]{2,1,0:T(8,128)(2,1)S(1)} %add_convert_fusion.3), channel_id=1, source_target_pairs={{0,8},{4,12},{8,16},{12,20},{16,24},{20,28},{24,0},{28,4},{1,9},{5... | collective-permute-start | bytes 884744 | tf_op jit(solution)/shard_map/ppermute | solution.py:298
where the time goes:
time: 138 us
  Pallas kernels  89.8 us (65%)
  waiting for transfers between devices  21.3 us (15%)
  starting transfers between devices  12.5 us (9%)
  matrix products  9.35 us (7%)
  other arithmetic  4.47 us (3%)
    pallas_call x1, Pallas kernels, filter_exchanged(): pl.pallas_call(functools.partial(exchange_kernel, lat_dev), out_shape=jax...  55.4 us
    pallas_call x8, Pallas kernels, synth_pair(): pl.pallas_call(synth_kernel, out_shape=(jax.ShapeDtypeStruct((1, lat_dev,...  34.4 us
    ppermute x6, waiting for transfers between devices, reduce_pairs(): here = lax.ppermute(here.astype(jnp.bfloat16), 'mem', onward)  21.3 us
    dot_general x1, matrix products, packed(): lax.dot_general(table, alpha.reshape(points, lon_count), (((1,), (1,)), (...  9.35 us
    ppermute x8, starting transfers between devices, reduce_pairs(): here = here + lax.ppermute(give, 'mem', swap).astype(jnp.float32)  8.03 us
    ppermute x6, starting transfers between devices, reduce_pairs(): here = lax.ppermute(here.astype(jnp.bfloat16), 'mem', onward)  4.46 us
  transfers between devices with their start and end apart: 14, of which 6 were waited for; matrix products, arithmetic and copies ran while one was open for 1% of the time, Pallas kernels for 22%

commit v1 on v0

v1 whole, which is shorter than its diff:
```python
import functools
import math

import jax
import jax.numpy as jnp
import numpy as np
from jax import lax
from jax.experimental import pallas as pl
from jax.experimental.pallas import tpu as pltpu
from jax.sharding import PartitionSpec as P


def build_table(lon_count, keep_dev, grid_count):
    col = np.arange(2 * keep_dev * grid_count)
    block = col // (2 * keep_dev)
    part = col // keep_dev % 2
    wave = block * keep_dev + col % keep_dev
    phase = wave[:, None] * np.arange(lon_count)[None, :] % lon_count
    angle = phase.astype(np.float32) * np.float32(2.0 * math.pi / lon_count)
    basis = np.where(part[:, None] == 0, np.cos(angle), np.sin(angle))
    return jnp.asarray(basis.astype(jnp.bfloat16))


def legendre_filter(split, legendre, response):
    coef = jnp.einsum("mnt,qmkit->qmkin", legendre, split, preferred_element_type=jnp.float32)
    coef = (coef * response[None, :, None, None, :]).astype(jnp.bfloat16)
    synth = jnp.einsum("mnt,qmkin->qmkit", legendre, coef, preferred_element_type=jnp.float32)
    return synth.astype(jnp.bfloat16)


def reduce_levels(partial, levels):
    mem_count = lax.axis_size("mem")
    me = lax.axis_index("mem")
    owned = levels // mem_count
    if mem_count % 2:
        every = jnp.concatenate([partial(i * owned, owned) for i in range(mem_count)])
        return lax.psum_scatter(every, "mem", scatter_dimension=0, tiled=True)
    ring = mem_count // 2
    side, place = me % 2, me // 2
    swap = [(j, j ^ 1) for j in range(mem_count)]
    onward = [(j, (j + 2) % mem_count) for j in range(mem_count)]
    total = None
    for step in range(ring):
        goal = (place + 2 * ring - 1 - step) % ring
        give = partial((2 * goal + 1 - side) * owned, owned).astype(jnp.bfloat16)
        got = lax.ppermute(give, "mem", swap)
        here = partial((2 * goal + side) * owned, owned)
        here = here + got.astype(jnp.float32)
        if total is not None:
            here = here + total.astype(jnp.float32)
        if step < ring - 1:
            total = lax.ppermute(here.astype(jnp.bfloat16), "mem", onward)
    return here


def wave_rows(rows_ref, wave, waves, lat_dev):
    grid_count, parts, depth, _ = rows_ref.shape
    tiles = depth // waves
    per_pair = 2 * lat_dev // 128
    pairs = tiles // per_pair
    half = per_pair // 2
    lines = []
    for part in range(parts):
        even, odd = [], []
        for src in range(grid_count):
            block = rows_ref[src, part, pl.ds(wave, tiles, stride=waves), :]
            piece = [block[i * pairs : (i + 1) * pairs] for i in range(per_pair)]
            even += piece[:half] + [piece[half][:, :64]]
            odd += [piece[half][:, 64:]] + piece[half + 1 :]
        lines += [jnp.concatenate(even, axis=1), jnp.concatenate(odd, axis=1)]
    return jnp.concatenate(lines, axis=0)


def wave_back(back_ref, synth, wave, waves, lat_dev):
    grid_count, parts, depth, _ = back_ref.shape
    tiles = depth // waves
    per_pair = 2 * lat_dev // 128
    pairs = tiles // per_pair
    for part in range(parts):
        even = synth[2 * part * pairs : (2 * part + 1) * pairs]
        odd = synth[(2 * part + 1) * pairs : (2 * part + 2) * pairs]
        for src in range(grid_count):
            base = src * lat_dev
            both = jnp.concatenate(
                [even[:, base : base + lat_dev], odd[:, base : base + lat_dev]], axis=1
            )
            block = jnp.concatenate(
                [both[:, i * 128 : (i + 1) * 128] for i in range(per_pair)], axis=0
            )
            back_ref[src, part, pl.ds(wave, tiles, stride=waves), :] = block


def filter_waves(lat_dev, waves, first, x_ref, legendre_ref, response_ref, out_ref, rows_ref, back_ref):
    grid_count, parts, depth, _ = rows_ref.shape
    tiles = depth // waves
    per_pair = 2 * lat_dev // 128
    pairs = tiles // per_pair
    span = pl.ds(first, waves)
    group = 4
    height = 2 * parts * pairs

    def spot(tile):
        return (tile % per_pair) * pairs + tile // per_pair

    for src in range(grid_count):
        for part in range(parts):
            for tile in range(tiles):
                rows_ref[src, part, spot(tile) * waves : (spot(tile) + 1) * waves, :] = x_ref[
                    src, part, span, tile * 128 : (tile + 1) * 128
                ].astype(jnp.float32)

    def one_group(step, carry):
        wave = step * group
        field = jnp.concatenate(
            [wave_rows(rows_ref, wave + i, waves, lat_dev) for i in range(group)], axis=0
        ).astype(jnp.bfloat16)
        basis = legendre_ref[pl.ds(first + wave, group)]
        degrees, lat_count = basis.shape[1:]
        every = lax.dot_general(
            field, basis.reshape(group * degrees, lat_count), (((1,), (1,)), ((), ())),
            preferred_element_type=jnp.float32,
        )
        for i in range(group):
            coef = every[i * height : (i + 1) * height, i * degrees : (i + 1) * degrees]
            coef = (coef * response_ref[pl.ds(first + wave + i, 1), :]).astype(jnp.bfloat16)
            synth = jnp.dot(coef, legendre_ref[first + wave + i], preferred_element_type=jnp.float32)
            wave_back(back_ref, synth, wave + i, waves, lat_dev)
        return carry

    lax.fori_loop(0, waves // group, one_group, 0, unroll=2)
    for src in range(grid_count):
        for part in range(parts):
            for tile in range(tiles):
                out_ref[src, part, span, tile * 128 : (tile + 1) * 128] = back_ref[
                    src, part, spot(tile) * waves : (spot(tile) + 1) * waves, :
                ].astype(jnp.bfloat16)


def whole_kernel(
    order, waves, strips, alpha_ref, pert_ref, legendre_ref, response_ref, table_ref, out_ref,
    table_v, alpha_v, pert_v, basis_v, weight_v, spec_v, taken_v, made_v, result_v, rows_v, back_v,
    give_v, got_v, keep_v, pass_v, come_v,
    table_sem, basis_sem, alpha_sem, pert_sem, out_send, out_recv, back_send, back_recv,
    x_send, x_recv, z_send, z_recv,
):
    chunks, grid_count, parts, keep_dev, points = spec_v.shape
    mem_dev, _, lat_dev, lon_count = alpha_v.shape[1:]
    cols = grid_count * parts * keep_dev
    subs = keep_dev // waves
    deep = lat_dev // strips
    mem_count = 2 * chunks
    g = lax.axis_index("grid")
    me = lax.axis_index("mem")
    side, place = me % 2, me // 2
    top = chunks - 1
    peers = [lax.rem(g + d, grid_count) for d in range(1, grid_count)]
    across = me + 1 - 2 * side
    above = lax.rem(me + 2, mem_count)
    below = lax.rem(me + mem_count - 2, mem_count)

    def local(src, dst, sem):
        return pltpu.make_async_copy(src, dst, sem)

    def remote(src, dst, send, recv, where):
        return pltpu.make_async_remote_copy(
            src_ref=src, dst_ref=dst, send_sem=send, recv_sem=recv,
            device_id=where, device_id_type=pl.DeviceIdType.MESH,
        )

    def alpha_copy(c):
        return local(alpha_ref.at[:, pl.ds(2 * order[c], 2)], alpha_v.at[c], alpha_sem.at[c])

    def pert_copy(c):
        return local(pert_ref.at[:, pl.ds(2 * order[c], 2)], pert_v.at[c], pert_sem.at[c])

    def basis_copy(s):
        span = pl.ds(s * waves, waves)
        return local(legendre_ref.at[span], basis_v.at[span], basis_sem.at[s])

    def out_copy(c, d):
        return remote(
            spec_v.at[c, peers[d]], taken_v.at[c, g], out_send.at[c, d], out_recv.at[c, d], {"grid": peers[d]}
        )

    def back_copy(c, s, d):
        span = pl.ds(pl.multiple_of(s * waves, waves), waves)
        return remote(
            made_v.at[c, peers[d], :, span], result_v.at[c, g, :, span],
            back_send.at[c, s, d], back_recv.at[c, s, d], {"grid": peers[d]},
        )

    def rows(s):
        return pl.ds(s * deep, deep)

    def x_copy(c, s):
        return remote(
            give_v.at[c, rows(s)], got_v.at[c, rows(s)], x_send.at[c, s], x_recv.at[c, s], {"mem": across}
        )

    def z_copy(c, s, up):
        way = 0 if up else 1
        return remote(
            pass_v.at[c, rows(s)], come_v.at[c, way, rows(s)], z_send.at[c, way, s], z_recv.at[c, way, s],
            {"mem": above if up else below},
        )

    local(table_ref, table_v, table_sem.at[0]).start()
    alpha_copy(0).start()
    barrier = pltpu.get_barrier_semaphore()
    for peer in peers:
        pl.semaphore_signal(barrier, inc=1, device_id={"grid": peer}, device_id_type=pl.DeviceIdType.MESH)
    pl.semaphore_signal(barrier, inc=1, device_id={"mem": across}, device_id_type=pl.DeviceIdType.MESH)

    @pl.when(place < top)
    def _():
        pl.semaphore_signal(barrier, inc=1, device_id={"mem": above}, device_id_type=pl.DeviceIdType.MESH)

    @pl.when(place > 0)
    def _():
        pl.semaphore_signal(barrier, inc=1, device_id={"mem": below}, device_id_type=pl.DeviceIdType.MESH)

    alpha_copy(1).start()
    for s in range(subs):
        basis_copy(s).start()
    for c in range(2, chunks):
        alpha_copy(c).start()
    for c in range(chunks):
        pert_copy(c).start()

    wave = lax.broadcasted_iota(jnp.int32, weight_v.shape, 0) + g * keep_dev
    weight_v[...] = response_ref[...] * jnp.where(wave == 0, 1.0, 2.0).astype(jnp.float32)

    def spectra(c):
        if c == 0:
            local(table_ref, table_v, table_sem.at[0]).wait()
        alpha_copy(c).wait()
        spec = lax.dot_general(
            table_v[...], alpha_v[c].reshape(points, lon_count), (((1,), (1,)), ((), ())),
            preferred_element_type=jnp.float32,
        ).astype(jnp.bfloat16)
        spec_v[c] = spec.reshape(grid_count, parts, keep_dev, points)

    def send_out(c):
        for d in range(grid_count - 1):
            out_copy(c, d).start()

    def legendre(c):
        for d in range(grid_count - 1):
            out_copy(c, d).wait_recv()
        taken_v[c, g] = spec_v[c, g]
        if c == 0:
            for s in range(subs):
                basis_copy(s).wait()

        def one(s, carry):
            filter_waves(
                lat_dev, waves, pl.multiple_of(s * waves, waves), taken_v.at[c], basis_v, weight_v,
                made_v.at[c], rows_v, back_v,
            )
            for d in range(grid_count - 1):
                back_copy(c, s, d).start()
            return carry

        lax.fori_loop(0, subs, one, 0)
        result_v[c, g] = made_v[c, g]

    def synth(c):
        pert_copy(c).wait()
        for s in range(subs):
            for d in range(grid_count - 1):
                back_copy(c, s, d).wait_recv()
        field = result_v[c].reshape(cols, points)
        wide = 256 if lon_count % 256 == 0 else lon_count
        for left in range(0, lon_count, wide):
            cut = slice(left, left + wide)
            both = [None, None]
            for k in range(mem_dev):
                values = lax.dot_general(
                    field[:, 2 * k * lat_dev : 2 * (k + 1) * lat_dev], table_v[:, cut],
                    (((0,), (0,)), ((), ())), preferred_element_type=jnp.float32,
                )
                for i in range(2):
                    term = values[i * lat_dev : (i + 1) * lat_dev] * pert_v[c, k, i, :, cut].astype(jnp.float32)
                    both[i] = term if k == 0 else both[i] + term
            give_v[c, :, cut] = jnp.where(side == 0, both[1], both[0]).astype(jnp.bfloat16)
            keep_v[c, :, cut] = jnp.where(side == 0, both[0], both[1])
        for s in range(strips):
            x_copy(c, s).start()

    def pair_up(c, s):
        x_copy(c, s).wait_recv()
        keep_v[c, rows(s)] = keep_v[c, rows(s)] + got_v[c, rows(s)].astype(jnp.float32)
        p = order[c]
        if p > 0:
            @pl.when(place == 0)
            def _():
                pass_v[c, rows(s)] = keep_v[c, rows(s)].astype(jnp.bfloat16)
                z_copy(c, s, True).start()
        if p < top:
            @pl.when(place == top)
            def _():
                pass_v[c, rows(s)] = keep_v[c, rows(s)].astype(jnp.bfloat16)
                z_copy(c, s, False).start()

    def line(c, s):
        p = order[c]

        def forward(up):
            z_copy(c, s, up).wait_recv()
            way = 0 if up else 1
            pass_v[c, rows(s)] = (
                keep_v[c, rows(s)] + come_v[c, way, rows(s)].astype(jnp.float32)
            ).astype(jnp.bfloat16)
            z_copy(c, s, up).start()

        if p > 1:
            @pl.when((place > 0) & (place < p))
            def _():
                forward(True)
        if p < top - 1:
            @pl.when((place > p) & (place < top))
            def _():
                forward(False)

        @pl.when(place == p)
        def _():
            total = keep_v[c, rows(s)]
            if p > 0:
                z_copy(c, s, True).wait_recv()
                total = total + come_v[c, 0, rows(s)].astype(jnp.float32)
            if p < top:
                z_copy(c, s, False).wait_recv()
                total = total + come_v[c, 1, rows(s)].astype(jnp.float32)
            out_ref[0, rows(s)] = total

    spectra(0)
    need = grid_count + (place < top).astype(jnp.int32) + (place > 0).astype(jnp.int32)
    pl.semaphore_wait(barrier, need)
    send_out(0)
    spectra(1)
    send_out(1)
    for c in range(2, chunks):
        spectra(c)
    for c in range(chunks):
        legendre(c)
        if c + 2 < chunks:
            send_out(c + 2)
        if c > 0:
            synth(c - 1)
        if c > 1:
            for s in range(strips):
                pair_up(c - 2, s)
    for c in range(chunks - 1, chunks):
        synth(c)
    for c in range(max(chunks - 2, 0)):
        for s in range(strips):
            line(c, s)
    for c in range(max(chunks - 2, 0), chunks):
        for s in range(strips):
            pair_up(c, s)
            line(c, s)
    for c in range(chunks):
        p = order[c]
        for d in range(grid_count - 1):
            out_copy(c, d).wait_send()
            for s in range(subs):
                back_copy(c, s, d).wait_send()
        for s in range(strips):
            x_copy(c, s).wait_send()
        if p > 0:
            @pl.when(place < p)
            def _():
                for s in range(strips):
                    z_copy(c, s, True).wait_send()
        if p < top:
            @pl.when(place > p)
            def _():
                for s in range(strips):
                    z_copy(c, s, False).wait_send()


def whole(alpha, perturbation, legendre, response, table):
    mem_dev, levels, lat_dev, lon_count = alpha.shape
    keep_dev, degrees, lat_count = legendre.shape
    cols = table.shape[0]
    grid_count = cols // (2 * keep_dev)
    chunks = levels // 2
    points = mem_dev * 2 * lat_dev
    waves = 16
    subs = keep_dev // waves
    strips = 2
    order = []
    for i in range((chunks + 1) // 2):
        order += [i] if i == chunks - 1 - i else [i, chunks - 1 - i]
    half, wide = jnp.bfloat16, jnp.float32
    fields = pltpu.VMEM((chunks, mem_dev, 2, lat_dev, lon_count), half)
    waved = pltpu.VMEM((chunks, grid_count, 2, keep_dev, points), half)
    turned = pltpu.VMEM((grid_count, 2, points // 128 * waves, 128), wide)
    level = (chunks, lat_dev, lon_count)
    dma = pltpu.SemaphoreType.DMA
    peers = grid_count - 1
    return pl.pallas_call(
        functools.partial(whole_kernel, order, waves, strips),
        out_shape=jax.ShapeDtypeStruct((1, lat_dev, lon_count), wide),
        in_specs=[
            pl.BlockSpec(memory_space=pl.ANY),
            pl.BlockSpec(memory_space=pl.ANY),
            pl.BlockSpec(memory_space=pl.ANY),
            pl.BlockSpec(memory_space=pltpu.VMEM),
            pl.BlockSpec(memory_space=pl.ANY),
        ],
        out_specs=pl.BlockSpec(memory_space=pltpu.VMEM),
        scratch_shapes=[
            pltpu.VMEM((cols, lon_count), half), fields, fields,
            pltpu.VMEM((keep_dev, degrees, lat_count), half), pltpu.VMEM((keep_dev, degrees), wide),
            waved, waved, waved, waved, turned, turned,
            pltpu.VMEM(level, half), pltpu.VMEM(level, half), pltpu.VMEM(level, wide), pltpu.VMEM(level, half),
            pltpu.VMEM((chunks, 2, lat_dev, lon_count), half),
            dma((1,)), dma((subs,)), dma((chunks,)), dma((chunks,)),
            dma((chunks, peers)), dma((chunks, peers)), dma((chunks, subs, peers)), dma((chunks, subs, peers)),
            dma((chunks, strips)), dma((chunks, strips)), dma((chunks, 2, strips)), dma((chunks, 2, strips)),
        ],
        compiler_params=pltpu.CompilerParams(
            vmem_limit_bytes=63 * 2**20, collective_id=0, has_side_effects=True
        ),
        cost_estimate=pl.CostEstimate(
            flops=2**35, bytes_accessed=2 * alpha.size, transcendentals=0
        ),
    )(alpha, perturbation, legendre, response, table)


def body(alpha, perturbation, legendre, response):
    mem_dev, levels, lat_dev, lon_count = alpha.shape
    keep_dev = legendre.shape[0]
    grid_count = lax.axis_size("grid")
    members = mem_dev * lax.axis_size("mem")
    cols = 2 * keep_dev
    table = build_table(lon_count, keep_dev, grid_count)
    scale = jnp.float32(1.0 / (lon_count * math.sqrt(members - 1)))
    if keep_dev % 16 == 0 and lat_dev % 128 == 64 and levels == lax.axis_size("mem") and levels in (4, 6, 8):
        return whole(alpha, perturbation, legendre, response, table) * scale

    wave = lax.axis_index("grid") * keep_dev + jnp.arange(keep_dev)
    response = response * jnp.where(wave == 0, 1.0, 2.0).astype(jnp.float32)[:, None]

    points = mem_dev * levels * lat_dev
    lane = math.gcd(points, 128)
    spectra = jnp.einsum("cx,klyx->ckly", table, alpha, preferred_element_type=jnp.float32)
    spectra = spectra.astype(jnp.bfloat16).reshape(grid_count, cols, points // lane, lane)
    spectra = lax.all_to_all(spectra, "grid", split_axis=0, concat_axis=0, tiled=True)
    split = spectra.reshape(grid_count, 2, keep_dev, mem_dev, levels, lat_dev)
    split = jnp.transpose(split, (1, 2, 3, 4, 0, 5)).reshape(2, keep_dev, mem_dev, levels, -1)
    filtered = legendre_filter(split, legendre, response)
    filtered = filtered.reshape(2, keep_dev, mem_dev, levels, grid_count, lat_dev)
    filtered = jnp.transpose(filtered, (4, 0, 1, 2, 3, 5)).reshape(grid_count, cols, points // lane, lane)
    filtered = lax.all_to_all(filtered, "grid", split_axis=0, concat_axis=0, tiled=True)
    filtered = filtered.reshape(grid_count * cols, mem_dev, levels, lat_dev)
    filtered = jnp.transpose(filtered, (1, 2, 3, 0))

    def partial(level, count):
        field = lax.dynamic_slice_in_dim(filtered, level, count, 1)
        weight = lax.dynamic_slice_in_dim(perturbation, level, count, 1)
        values = jnp.einsum("klyc,cx->klyx", field, table, preferred_element_type=jnp.float32)
        return jnp.sum(values * weight, axis=0)

    total = reduce_levels(partial, levels)
    return total * scale


def solution(mesh):
    placed = (
        P("mem", None, "grid", None),
        P("mem", None, "grid", None),
        P("grid", None, None),
        P("grid", None),
    )
    return jax.shard_map(
        body, mesh=mesh, in_specs=placed, out_specs=P("mem", "grid", None), check_vma=False
    )
```

time: 138 us -> 133 us (0.964)
  the two profiles are of different devices: /device:TPU:0 before, /device:TPU:16 now
where the time goes in v1:
time: 133 us
  Pallas kernels  130 us (98%)
  other arithmetic  2.39 us (2%)
    pallas_call x1, Pallas kernels, whole(): pl.pallas_call(functools.partial(whole_kernel, order, waves, strips), out...  130 us

profile of v1, /device:TPU:16, one launch (start us, length us, event | category | flops | bytes accessed | tf_op | source)
XLA Modules:
  0.0 132.8 jit_solution(8714827899307018375)
XLA Ops:
  0.0 130.4 %shard_map.55 = f32[1,192,1536]{2,1,0:T(8,128)} custom-call(bf16[2,8,192,1536]{3,2,1,0:T(8,128)(2,1)} %alpha_ref.1, bf16[2,8,192,1536]{3,2,1,0:T(8,128)(2,1)} %pert_ref.1, bf16[48,128,768]{2,1,0:T(8,128)(2,1)} %legendre_ref.1, f32[48,128]{1,0:T(8,128)} %response_ref.1, bf16[384,1536]{1,0:T(8,128)(2,1)} %constant.4.clone.table_ref), custom_call_target="tpu_custom_call" | custom-call | flops 34359738368 | bytes 9437184 | tf_op jit(solution)/shard_map/pallas_call | solution.py:402
  130.5 2.4 %broadcast_multiply_fusion = f32[1,192,1536]{2,1,0:T(8,128)} fusion(f32[1,192,1536]{2,1,0:T(8,128)} %shard_map.55), kind=kLoop, calls=%fused_computation | loop fusion | flops 294912 | bytes 2359296 | tf_op jit(solution)/shard_map/mul | solution.py:441

commit v2 on v1

--- a/solution.py
+++ b/solution.py
@@ -168,7 +168,7 @@
         )
 
     def alpha_copy(c):
-        return local(alpha_ref.at[:, pl.ds(2 * order[c], 2)], alpha_v.at[c], alpha_sem.at[c])
+        return local(alpha_ref.at[:, pl.ds(2 * order[c], 2)], alpha_v.at[c % 2], alpha_sem.at[c])
 
     def pert_copy(c):
         return local(pert_ref.at[:, pl.ds(2 * order[c], 2)], pert_v.at[c], pert_sem.at[c])
@@ -177,13 +177,15 @@
         span = pl.ds(s * waves, waves)
         return local(legendre_ref.at[span], basis_v.at[span], basis_sem.at[s])
 
-    def out_copy(c, d):
+    def out_copy(c, s, d):
+        span = pl.ds(s * waves, waves)
         return remote(
-            spec_v.at[c, peers[d]], taken_v.at[c, g], out_send.at[c, d], out_recv.at[c, d], {"grid": peers[d]}
+            spec_v.at[c, peers[d], :, span], taken_v.at[c, g, :, span],
+            out_send.at[c, s, d], out_recv.at[c, s, d], {"grid": peers[d]},
         )
 
     def back_copy(c, s, d):
-        span = pl.ds(pl.multiple_of(s * waves, waves), waves)
+        span = pl.ds(s * waves, waves)
         return remote(
             made_v.at[c, peers[d], :, span], result_v.at[c, g, :, span],
             back_send.at[c, s, d], back_recv.at[c, s, d], {"grid": peers[d]},
@@ -219,50 +221,48 @@
     def _():
         pl.semaphore_signal(barrier, inc=1, device_id={"mem": below}, device_id_type=pl.DeviceIdType.MESH)
 
+    local(response_ref, weight_v, table_sem.at[1]).start()
     alpha_copy(1).start()
-    for s in range(subs):
-        basis_copy(s).start()
-    for c in range(2, chunks):
-        alpha_copy(c).start()
-    for c in range(chunks):
-        pert_copy(c).start()
-
-    wave = lax.broadcasted_iota(jnp.int32, weight_v.shape, 0) + g * keep_dev
-    weight_v[...] = response_ref[...] * jnp.where(wave == 0, 1.0, 2.0).astype(jnp.float32)
 
     def spectra(c):
         if c == 0:
             local(table_ref, table_v, table_sem.at[0]).wait()
         alpha_copy(c).wait()
+        if c == 0:
+            for s in range(subs):
+                basis_copy(s).start()
         spec = lax.dot_general(
-            table_v[...], alpha_v[c].reshape(points, lon_count), (((1,), (1,)), ((), ())),
+            table_v[...], alpha_v[c % 2].reshape(points, lon_count), (((1,), (1,)), ((), ())),
             preferred_element_type=jnp.float32,
         ).astype(jnp.bfloat16)
         spec_v[c] = spec.reshape(grid_count, parts, keep_dev, points)
+        taken_v[c, g] = spec_v[c, g]
+        if c + 2 < chunks:
+            alpha_copy(c + 2).start()
 
     def send_out(c):
+        for s in range(subs):
+            for d in range(grid_count - 1):
+                out_copy(c, s, d).start()
+
+    def legendre(c, s):
+        if c == 0:
+            basis_copy(s).wait()
+            pert_copy(s).start()
+            if s == subs - 1:
+                for other in range(subs, chunks):
+                    pert_copy(other).start()
         for d in range(grid_count - 1):
-            out_copy(c, d).start()
-
-    def legendre(c):
+            out_copy(c, s, d).wait_recv()
+        filter_waves(
+            lat_dev, waves, s * waves, taken_v.at[c], basis_v, weight_v, made_v.at[c], rows_v, back_v
+        )
         for d in range(grid_count - 1):
-            out_copy(c, d).wait_recv()
-        taken_v[c, g] = spec_v[c, g]
-        if c == 0:
-            for s in range(subs):
-                basis_copy(s).wait()
-
-        def one(s, carry):
-            filter_waves(
-                lat_dev, waves, pl.multiple_of(s * waves, waves), taken_v.at[c], basis_v, weight_v,
-                made_v.at[c], rows_v, back_v,
-            )
-            for d in range(grid_count - 1):
-                back_copy(c, s, d).start()
-            return carry
-
-        lax.fori_loop(0, subs, one, 0)
-        result_v[c, g] = made_v[c, g]
+            back_copy(c, s, d).start()
+        if s == subs - 1:
+            if c + 1 < chunks:
+                send_out(c + 1)
+            result_v[c, g] = made_v[c, g]
 
     def synth(c):
         pert_copy(c).wait()
@@ -287,83 +287,57 @@
         for s in range(strips):
             x_copy(c, s).start()
 
-    def pair_up(c, s):
+    def gather(c, s, z):
+        p = order[c]
         x_copy(c, s).wait_recv()
-        keep_v[c, rows(s)] = keep_v[c, rows(s)] + got_v[c, rows(s)].astype(jnp.float32)
+        total = keep_v[c, rows(s)] + got_v[c, rows(s)].astype(jnp.float32)
+        for way in range(2):
+            up = way == 0
+            if (0 < z <= p) if up else (p <= z < top):
+                z_copy(c, s, up).wait_recv()
+                total = total + come_v[c, way, rows(s)].astype(jnp.float32)
+        if z == p:
+            out_ref[0, rows(s)] = total
+        else:
+            pass_v[c, rows(s)] = total.astype(jnp.bfloat16)
+            z_copy(c, s, z < p).start()
+
+    steps = []
+    for c in range(chunks):
         p = order[c]
-        if p > 0:
-            @pl.when(place == 0)
-            def _():
-                pass_v[c, rows(s)] = keep_v[c, rows(s)].astype(jnp.bfloat16)
-                z_copy(c, s, True).start()
-        if p < top:
-            @pl.when(place == top)
-            def _():
-                pass_v[c, rows(s)] = keep_v[c, rows(s)].astype(jnp.bfloat16)
-                z_copy(c, s, False).start()
-
-    def line(c, s):
-        p = order[c]
-
-        def forward(up):
-            z_copy(c, s, up).wait_recv()
-            way = 0 if up else 1
-            pass_v[c, rows(s)] = (
-                keep_v[c, rows(s)] + come_v[c, way, rows(s)].astype(jnp.float32)
-            ).astype(jnp.bfloat16)
-            z_copy(c, s, up).start()
-
-        if p > 1:
-            @pl.when((place > 0) & (place < p))
-            def _():
-                forward(True)
-        if p < top - 1:
-            @pl.when((place > p) & (place < top))
-            def _():
-                forward(False)
-
-        @pl.when(place == p)
-        def _():
-            total = keep_v[c, rows(s)]
-            if p > 0:
-                z_copy(c, s, True).wait_recv()
-                total = total + come_v[c, 0, rows(s)].astype(jnp.float32)
-            if p < top:
-                z_copy(c, s, False).wait_recv()
-                total = total + come_v[c, 1, rows(s)].astype(jnp.float32)
-            out_ref[0, rows(s)] = total
+        begin = 12.8 * c
+        steps += [(8.4 + begin + 2.2 * s, legendre, (c, s)) for s in range(subs)]
+        steps.append((19.1 + begin, synth, (c,)))
+        if c > 0:
+            steps.append((3.0 + 6.3 * c, spectra, (c,)))
+        for z in range(chunks):
+            hops = z if z < p else top - z if z > p else max(p, top - p)
+            slack = 0.0 if c == chunks - 1 else 1.5
+            for s in range(strips):
+                ready = 23.0 + slack + begin + 12.7 * (s + 1) / strips + hops * (2.8 + slack + 12.7 / strips)
+                steps.append((ready, gather, (c, s, z)))
+    steps.sort(key=lambda step: step[0])
 
     spectra(0)
+    local(response_ref, weight_v, table_sem.at[1]).wait()
+    wave = lax.broadcasted_iota(jnp.int32, weight_v.shape, 0) + g * keep_dev
+    weight_v[...] = weight_v[...] * jnp.where(wave == 0, 1.0, 2.0).astype(jnp.float32)
     need = grid_count + (place < top).astype(jnp.int32) + (place > 0).astype(jnp.int32)
     pl.semaphore_wait(barrier, need)
     send_out(0)
-    spectra(1)
-    send_out(1)
-    for c in range(2, chunks):
-        spectra(c)
-    for c in range(chunks):
-        legendre(c)
-        if c + 2 < chunks:
-            send_out(c + 2)
-        if c > 0:
-            synth(c - 1)
-        if c > 1:
-            for s in range(strips):
-                pair_up(c - 2, s)
-    for c in range(chunks - 1, chunks):
-        synth(c)
-    for c in range(max(chunks - 2, 0)):
-        for s in range(strips):
-            line(c, s)
-    for c in range(max(chunks - 2, 0), chunks):
-        for s in range(strips):
-            pair_up(c, s)
-            line(c, s)
+    steps = [step for step in steps if step[1] is spectra and step[2] == (1,)] + [
+        step for step in steps if not (step[1] is spectra and step[2] == (1,))
+    ]
+    for _, act, which in steps:
+        if act is gather:
+            pl.when(place == which[2])(functools.partial(gather, *which))
+        else:
+            act(*which)
     for c in range(chunks):
         p = order[c]
         for d in range(grid_count - 1):
-            out_copy(c, d).wait_send()
             for s in range(subs):
+                out_copy(c, s, d).wait_send()
                 back_copy(c, s, d).wait_send()
         for s in range(strips):
             x_copy(c, s).wait_send()
@@ -388,12 +362,10 @@
     points = mem_dev * 2 * lat_dev
     waves = 16
     subs = keep_dev // waves
-    strips = 2
-    order = []
-    for i in range((chunks + 1) // 2):
-        order += [i] if i == chunks - 1 - i else [i, chunks - 1 - i]
+    strips = 4
+    order = list(range(1, chunks, 2)) + list(range(0, chunks, 2))
     half, wide = jnp.bfloat16, jnp.float32
-    fields = pltpu.VMEM((chunks, mem_dev, 2, lat_dev, lon_count), half)
+    field = (mem_dev, 2, lat_dev, lon_count)
     waved = pltpu.VMEM((chunks, grid_count, 2, keep_dev, points), half)
     turned = pltpu.VMEM((grid_count, 2, points // 128 * waves, 128), wide)
     level = (chunks, lat_dev, lon_count)
@@ -406,22 +378,22 @@
             pl.BlockSpec(memory_space=pl.ANY),
             pl.BlockSpec(memory_space=pl.ANY),
             pl.BlockSpec(memory_space=pl.ANY),
-            pl.BlockSpec(memory_space=pltpu.VMEM),
+            pl.BlockSpec(memory_space=pl.ANY),
             pl.BlockSpec(memory_space=pl.ANY),
         ],
         out_specs=pl.BlockSpec(memory_space=pltpu.VMEM),
         scratch_shapes=[
-            pltpu.VMEM((cols, lon_count), half), fields, fields,
+            pltpu.VMEM((cols, lon_count), half), pltpu.VMEM((2,) + field, half), pltpu.VMEM((chunks,) + field, half),
             pltpu.VMEM((keep_dev, degrees, lat_count), half), pltpu.VMEM((keep_dev, degrees), wide),
             waved, waved, waved, waved, turned, turned,
             pltpu.VMEM(level, half), pltpu.VMEM(level, half), pltpu.VMEM(level, wide), pltpu.VMEM(level, half),
             pltpu.VMEM((chunks, 2, lat_dev, lon_count), half),
-            dma((1,)), dma((subs,)), dma((chunks,)), dma((chunks,)),
-            dma((chunks, peers)), dma((chunks, peers)), dma((chunks, subs, peers)), dma((chunks, subs, peers)),
+            dma((2,)), dma((subs,)), dma((chunks,)), dma((chunks,)),
+            dma((chunks, subs, peers)), dma((chunks, subs, peers)), dma((chunks, subs, peers)), dma((chunks, subs, peers)),
             dma((chunks, strips)), dma((chunks, strips)), dma((chunks, 2, strips)), dma((chunks, 2, strips)),
         ],
         compiler_params=pltpu.CompilerParams(
-            vmem_limit_bytes=63 * 2**20, collective_id=0, has_side_effects=True
+            vmem_limit_bytes=53 * 2**20, collective_id=0, has_side_effects=True
         ),
         cost_estimate=pl.CostEstimate(
             flops=2**35, bytes_accessed=2 * alpha.size, transcendentals=0

time: 133 us -> 90.2 us (0.68)
  Pallas kernels: 130 us -> 86.8 us
    pallas_call x1, Pallas kernels: 130 us -> 86.8 us  [whole(): pl.pallas_call(functools.partial(whole_kernel, order, waves, strips), out...]
where the time goes in v2:
time: 90.2 us; the launch traced here: 90 us
  Pallas kernels  86.8 us (96%)
  other arithmetic  2.39 us (3%)
    pallas_call x1, Pallas kernels, whole(): pl.pallas_call(functools.partial(whole_kernel, order, waves, strips), out...  86.8 us
    mul x1, other arithmetic, body(): return whole(alpha, perturbation, legendre, response, table) * scale  2.39 us

profile of v2, /device:TPU:16, one launch (start us, length us, event | category | flops | bytes accessed | tf_op | source)
XLA Modules:
  0.0 90.0 jit_solution(11656946778232659711)
XLA Ops:
  0.0 0.0 copy-start
  0.0 0.7 copy-done
  0.7 86.8 %shard_map.55 = f32[1,192,1536]{2,1,0:T(8,128)} custom-call(bf16[2,8,192,1536]{3,2,1,0:T(8,128)(2,1)} %alpha_ref.1, bf16[2,8,192,1536]{3,2,1,0:T(8,128)(2,1)} %pert_ref.1, bf16[48,128,768]{2,1,0:T(8,128)(2,1)} %legendre_ref.1, f32[48,128]{1,0:T(8,128)S(1)} %copy-done, bf16[384,1536]{1,0:T(8,128)(2,1)} %constant.4.clone.table_ref), custom_call_target="tpu_custom_call" | custom-call | flops 34359738368 | bytes 9437184 | tf_op jit(solution)/shard_map/pallas_call | solution.py:374
  87.6 2.4 %broadcast_multiply_fusion = f32[1,192,1536]{2,1,0:T(8,128)} fusion(f32[1,192,1536]{2,1,0:T(8,128)} %shard_map.55), kind=kLoop, calls=%fused_computation | loop fusion | flops 294912 | bytes 2359296 | tf_op jit(solution)/shard_map/mul | solution.py:413
Async XLA Ops:
  0.0 0.7 copy-start

commit v3 on v2

--- a/solution.py
+++ b/solution.py
@@ -139,15 +139,14 @@
 def whole_kernel(
     order, waves, strips, alpha_ref, pert_ref, legendre_ref, response_ref, table_ref, out_ref,
     table_v, alpha_v, pert_v, basis_v, weight_v, spec_v, taken_v, made_v, result_v, rows_v, back_v,
-    give_v, got_v, keep_v, pass_v, come_v,
-    table_sem, basis_sem, alpha_sem, pert_sem, out_send, out_recv, back_send, back_recv,
-    x_send, x_recv, z_send, z_recv,
+    give_v, got_v, keep_v, pass_v, come_v, done_v,
+    table_sem, first_sem, basis_sem, alpha_sem, pert_sem, out_send, out_recv, back_send, back_recv,
+    x_send, x_recv, z_send, z_recv, done_sem,
 ):
     chunks, grid_count, parts, keep_dev, points = spec_v.shape
     mem_dev, _, lat_dev, lon_count = alpha_v.shape[1:]
     cols = grid_count * parts * keep_dev
     subs = keep_dev // waves
-    deep = lat_dev // strips
     mem_count = 2 * chunks
     g = lax.axis_index("grid")
     me = lax.axis_index("mem")
@@ -170,6 +169,9 @@
     def alpha_copy(c):
         return local(alpha_ref.at[:, pl.ds(2 * order[c], 2)], alpha_v.at[c % 2], alpha_sem.at[c])
 
+    def first_copy(k):
+        return local(alpha_ref.at[k, pl.ds(2 * order[0], 2)], alpha_v.at[0, k], first_sem.at[k])
+
     def pert_copy(c):
         return local(pert_ref.at[:, pl.ds(2 * order[c], 2)], pert_v.at[c], pert_sem.at[c])
 
@@ -191,23 +193,28 @@
             back_send.at[c, s, d], back_recv.at[c, s, d], {"grid": peers[d]},
         )
 
-    def rows(s):
+    def rows(c, s):
+        deep = lat_dev // strips[c]
         return pl.ds(s * deep, deep)
 
     def x_copy(c, s):
         return remote(
-            give_v.at[c, rows(s)], got_v.at[c, rows(s)], x_send.at[c, s], x_recv.at[c, s], {"mem": across}
+            give_v.at[c, rows(c, s)], got_v.at[c, rows(c, s)], x_send.at[c, s], x_recv.at[c, s], {"mem": across}
         )
 
     def z_copy(c, s, up):
         way = 0 if up else 1
         return remote(
-            pass_v.at[c, rows(s)], come_v.at[c, way, rows(s)], z_send.at[c, way, s], z_recv.at[c, way, s],
+            pass_v.at[c, rows(c, s)], come_v.at[c, way, rows(c, s)], z_send.at[c, way, s], z_recv.at[c, way, s],
             {"mem": above if up else below},
         )
 
+    def done_copy(c, s):
+        return local(done_v.at[rows(c, s)], out_ref.at[0, rows(c, s)], done_sem.at[s])
+
     local(table_ref, table_v, table_sem.at[0]).start()
-    alpha_copy(0).start()
+    for k in range(mem_dev):
+        first_copy(k).start()
     barrier = pltpu.get_barrier_semaphore()
     for peer in peers:
         pl.semaphore_signal(barrier, inc=1, device_id={"grid": peer}, device_id_type=pl.DeviceIdType.MESH)
@@ -222,20 +229,31 @@
         pl.semaphore_signal(barrier, inc=1, device_id={"mem": below}, device_id_type=pl.DeviceIdType.MESH)
 
     local(response_ref, weight_v, table_sem.at[1]).start()
-    alpha_copy(1).start()
 
     def spectra(c):
         if c == 0:
             local(table_ref, table_v, table_sem.at[0]).wait()
-        alpha_copy(c).wait()
-        if c == 0:
+            lanes = points // mem_dev
+            for k in range(mem_dev):
+                first_copy(k).wait()
+                if k == mem_dev - 1:
+                    alpha_copy(1).start()
+                spec = lax.dot_general(
+                    table_v[...], alpha_v[0, k].reshape(lanes, lon_count), (((1,), (1,)), ((), ())),
+                    preferred_element_type=jnp.float32,
+                ).astype(jnp.bfloat16)
+                spec_v[0, :, :, :, k * lanes : (k + 1) * lanes] = spec.reshape(
+                    grid_count, parts, keep_dev, lanes
+                )
             for s in range(subs):
                 basis_copy(s).start()
-        spec = lax.dot_general(
-            table_v[...], alpha_v[c % 2].reshape(points, lon_count), (((1,), (1,)), ((), ())),
-            preferred_element_type=jnp.float32,
-        ).astype(jnp.bfloat16)
-        spec_v[c] = spec.reshape(grid_count, parts, keep_dev, points)
+        else:
+            alpha_copy(c).wait()
+            spec = lax.dot_general(
+                table_v[...], alpha_v[c % 2].reshape(points, lon_count), (((1,), (1,)), ((), ())),
+                preferred_element_type=jnp.float32,
+            ).astype(jnp.bfloat16)
+            spec_v[c] = spec.reshape(grid_count, parts, keep_dev, points)
         taken_v[c, g] = spec_v[c, g]
         if c + 2 < chunks:
             alpha_copy(c + 2).start()
@@ -264,8 +282,39 @@
                 send_out(c + 1)
             result_v[c, g] = made_v[c, g]
 
+    def settle_grid(c):
+        for s in range(subs):
+            for d in range(grid_count - 1):
+                out_copy(c, s, d).wait_send()
+                back_copy(c, s, d).wait_send()
+
+    def settle_pair(c):
+        for s in range(strips[c]):
+            x_copy(c, s).wait_send()
+
+    def settle_line(c):
+        p = order[c]
+
+        def sent(up):
+            for s in range(strips[c]):
+                z_copy(c, s, up).wait_send()
+
+        @pl.when(place == p)
+        def _():
+            for s in range(strips[c]):
+                done_copy(c, s).wait()
+
+        if p > 0:
+            pl.when(place < p)(functools.partial(sent, True))
+        if p < top:
+            pl.when(place > p)(functools.partial(sent, False))
+
     def synth(c):
         pert_copy(c).wait()
+        if c > 0:
+            settle_grid(c - 1)
+        if c > 1:
+            settle_pair(c - 2)
         for s in range(subs):
             for d in range(grid_count - 1):
                 back_copy(c, s, d).wait_recv()
@@ -284,22 +333,25 @@
                     both[i] = term if k == 0 else both[i] + term
             give_v[c, :, cut] = jnp.where(side == 0, both[1], both[0]).astype(jnp.bfloat16)
             keep_v[c, :, cut] = jnp.where(side == 0, both[0], both[1])
-        for s in range(strips):
+        for s in range(strips[c]):
             x_copy(c, s).start()
+        if c == top:
+            settle_grid(c)
 
     def gather(c, s, z):
         p = order[c]
         x_copy(c, s).wait_recv()
-        total = keep_v[c, rows(s)] + got_v[c, rows(s)].astype(jnp.float32)
+        total = keep_v[c, rows(c, s)] + got_v[c, rows(c, s)].astype(jnp.float32)
         for way in range(2):
             up = way == 0
             if (0 < z <= p) if up else (p <= z < top):
                 z_copy(c, s, up).wait_recv()
-                total = total + come_v[c, way, rows(s)].astype(jnp.float32)
+                total = total + come_v[c, way, rows(c, s)].astype(jnp.float32)
         if z == p:
-            out_ref[0, rows(s)] = total
+            done_v[rows(c, s)] = total
+            done_copy(c, s).start()
         else:
-            pass_v[c, rows(s)] = total.astype(jnp.bfloat16)
+            pass_v[c, rows(c, s)] = total.astype(jnp.bfloat16)
             z_copy(c, s, z < p).start()
 
     steps = []
@@ -312,10 +364,15 @@
             steps.append((3.0 + 6.3 * c, spectra, (c,)))
         for z in range(chunks):
             hops = z if z < p else top - z if z > p else max(p, top - p)
-            slack = 0.0 if c == chunks - 1 else 1.5
-            for s in range(strips):
-                ready = 23.0 + slack + begin + 12.7 * (s + 1) / strips + hops * (2.8 + slack + 12.7 / strips)
+            slack = [0.0, 0.5, 1.5][min(top - c, 2)]
+            for s in range(strips[c]):
+                wire = 12.7 / strips[c]
+                ready = 23.0 + slack + begin + wire * (s + 1) + hops * (2.8 + slack + wire)
                 steps.append((ready, gather, (c, s, z)))
+        if c < top:
+            last = max(step[0] for step in steps if step[1] is gather and step[2][0] == c)
+            steps.append((last + 3.0, settle_line, (c,)))
+    steps.append((26.0 + 12.8 * top, settle_pair, (top - 1,)))
     steps.sort(key=lambda step: step[0])
 
     spectra(0)
@@ -333,24 +390,8 @@
             pl.when(place == which[2])(functools.partial(gather, *which))
         else:
             act(*which)
-    for c in range(chunks):
-        p = order[c]
-        for d in range(grid_count - 1):
-            for s in range(subs):
-                out_copy(c, s, d).wait_send()
-                back_copy(c, s, d).wait_send()
-        for s in range(strips):
-            x_copy(c, s).wait_send()
-        if p > 0:
-            @pl.when(place < p)
-            def _():
-                for s in range(strips):
-                    z_copy(c, s, True).wait_send()
-        if p < top:
-            @pl.when(place > p)
-            def _():
-                for s in range(strips):
-                    z_copy(c, s, False).wait_send()
+    settle_pair(top)
+    settle_line(top)
 
 
 def whole(alpha, perturbation, legendre, response, table):
@@ -362,7 +403,8 @@
     points = mem_dev * 2 * lat_dev
     waves = 16
     subs = keep_dev // waves
-    strips = 4
+    strips = [4] * (chunks - 1) + [6]
+    most = max(strips)
     order = list(range(1, chunks, 2)) + list(range(0, chunks, 2))
     half, wide = jnp.bfloat16, jnp.float32
     field = (mem_dev, 2, lat_dev, lon_count)
@@ -381,16 +423,17 @@
             pl.BlockSpec(memory_space=pl.ANY),
             pl.BlockSpec(memory_space=pl.ANY),
         ],
-        out_specs=pl.BlockSpec(memory_space=pltpu.VMEM),
+        out_specs=pl.BlockSpec(memory_space=pl.ANY),
         scratch_shapes=[
             pltpu.VMEM((cols, lon_count), half), pltpu.VMEM((2,) + field, half), pltpu.VMEM((chunks,) + field, half),
             pltpu.VMEM((keep_dev, degrees, lat_count), half), pltpu.VMEM((keep_dev, degrees), wide),
             waved, waved, waved, waved, turned, turned,
             pltpu.VMEM(level, half), pltpu.VMEM(level, half), pltpu.VMEM(level, wide), pltpu.VMEM(level, half),
-            pltpu.VMEM((chunks, 2, lat_dev, lon_count), half),
-            dma((2,)), dma((subs,)), dma((chunks,)), dma((chunks,)),
+            pltpu.VMEM((chunks, 2, lat_dev, lon_count), half), pltpu.VMEM((lat_dev, lon_count), wide),
+            dma((2,)), dma((mem_dev,)), dma((subs,)), dma((chunks,)), dma((chunks,)),
             dma((chunks, subs, peers)), dma((chunks, subs, peers)), dma((chunks, subs, peers)), dma((chunks, subs, peers)),
-            dma((chunks, strips)), dma((chunks, strips)), dma((chunks, 2, strips)), dma((chunks, 2, strips)),
+            dma((chunks, most)), dma((chunks, most)), dma((chunks, 2, most)), dma((chunks, 2, most)),
+            dma((most,)),
         ],
         compiler_params=pltpu.CompilerParams(
             vmem_limit_bytes=53 * 2**20, collective_id=0, has_side_effects=True

time: 90.2 us -> 89.6 us (level)
  no operation moved by 1% of the time
where the time goes in v3:
time: 89.6 us; the launch traced here: 89.4 us
  Pallas kernels  86.2 us (96%)
  other arithmetic  2.39 us (3%)
    pallas_call x1, Pallas kernels, whole(): pl.pallas_call(functools.partial(whole_kernel, order, waves, strips), out...  86.2 us
    mul x1, other arithmetic, body(): return whole(alpha, perturbation, legendre, response, table) * scale  2.39 us

profile of v3, /device:TPU:16, one launch (start us, length us, event | category | flops | bytes accessed | tf_op | source)
XLA Modules:
  0.0 89.4 jit_solution(14173214912848394862)
XLA Ops:
  0.0 0.0 copy-start
  0.0 0.7 copy-done
  0.7 86.2 %shard_map.55 = f32[1,192,1536]{2,1,0:T(8,128)} custom-call(bf16[2,8,192,1536]{3,2,1,0:T(8,128)(2,1)} %alpha_ref.1, bf16[2,8,192,1536]{3,2,1,0:T(8,128)(2,1)} %pert_ref.1, bf16[48,128,768]{2,1,0:T(8,128)(2,1)} %legendre_ref.1, f32[48,128]{1,0:T(8,128)S(1)} %copy-done, bf16[384,1536]{1,0:T(8,128)(2,1)} %constant.4.clone.table_ref), custom_call_target="tpu_custom_call" | custom-call | flops 34359738368 | bytes 9437184 | tf_op jit(solution)/shard_map/pallas_call | solution.py:416
  87.0 2.4 %broadcast_multiply_fusion = f32[1,192,1536]{2,1,0:T(8,128)} fusion(f32[1,192,1536]{2,1,0:T(8,128)} %shard_map.55), kind=kLoop, calls=%fused_computation | loop fusion | flops 294912 | bytes 2359296 | tf_op jit(solution)/shard_map/mul | solution.py:456
Async XLA Ops:
  0.0 0.7 copy-start
